TPU v7x, 32 devices: a whole 2x2x4 slice. The times are simulated.
32 devices in a mesh: rep: 4 (over x, core), shard: 8 (over z, y).
Axes of the slice: x: 2, y: 2, z: 4, core: 2. Of those that a mesh axis runs over, the one named last changes fastest.
Arguments:
- dense_out: bfloat16 [4096, 128], P(('rep', 'shard')), may hold values from -0.75 to 0.75
- pooled: bfloat16 [4096, 26, 128], P(('rep', 'shard')), may hold values from -0.75 to 0.75
- top_weight: bfloat16 [479, 1024], replicated, may hold values from -0.25 to 0.25
- top_cotangent: bfloat16 [4096, 1024], P(('rep', 'shard')), may hold values from -3 to 3
- indices: int32 [4096, 26, 2], P(('rep', 'shard')), may hold values from 0 to 2047, as said below
Outputs:
- dense_grad: bfloat16 [4096, 128], P(('rep', 'shard'))
- top_grad: float32 [479, 1024], replicated
- bias_grad: float32 [1024], replicated
- table_grad: float32 [26, 2048, 128], P(None, 'shard')
Inputs may be any that keep to these rules, and one draw needn't show every extreme that they name: `indices`: rows r with r // 256 = s are held by shard s. For every device's 128 samples and every table, at most 16 of the device's lookups fall in any one block of 64 rows starting at a multiple of 64, and some such block holds exactly 16.
All inputs are finite; a program needn't handle non-finite values.
Results may differ from a plain program's by a relative error of at most 0.008.
Values may be sent and summed in bfloat16 or wider, within the bound.
A program may use at most 128 MiB of HBM per device.

v0:
```python
import jax
import jax.numpy as jnp
import numpy as np
from jax import lax
from jax.sharding import PartitionSpec as P

R_SHARD = 256
highest = lax.Precision.HIGHEST


def one_hot_sums(rows, keys, height):
    tables_here = rows.shape[0]
    flat_rows = rows.reshape(tables_here, -1, rows.shape[-1])
    flat_keys = keys.reshape(tables_here, -1)

    def per_table(member):
        table_rows, table_keys = member
        levels = lax.broadcasted_iota(jnp.int32, (height, table_keys.shape[0]), 0)
        matches = (levels == table_keys[None, :]).astype(jnp.bfloat16)
        return jnp.dot(matches, table_rows, preferred_element_type=jnp.float32)

    return lax.map(per_table, (flat_rows, flat_keys))


def pair_table(vectors):
    lower_i, lower_j = np.tril_indices(vectors, -1)
    select = np.zeros((vectors * vectors, lower_i.shape[0]), np.float32)
    select[lower_i * vectors + lower_j, np.arange(lower_i.shape[0])] = 1.0
    mirrored = np.zeros((lower_i.shape[0], vectors * vectors), np.float32)
    mirrored[np.arange(lower_i.shape[0]), lower_i * vectors + lower_j] = 1.0
    mirrored[np.arange(lower_i.shape[0]), lower_j * vectors + lower_i] = 1.0
    return (jnp.asarray(select), jnp.asarray(mirrored))


def on_device(dense_out, pooled, top_weight, top_cotangent, indices):
    samples = dense_out.shape[0]
    emb_width = dense_out.shape[1]
    tables = pooled.shape[1]
    lookups = indices.shape[2]
    replicas = lax.axis_size("rep")
    shards = lax.axis_size("shard")
    vectors = tables + 1
    select, mirrored = pair_table(vectors)
    stacked = jnp.concatenate([dense_out[:, None, :], pooled], axis=1)
    gram_matrix = jnp.einsum("bie,bje->bij", stacked, stacked, preferred_element_type=jnp.float32)
    gram_flat = gram_matrix.reshape(samples, vectors * vectors)
    pair_values = jnp.dot(
        gram_flat, select, precision=highest, preferred_element_type=jnp.float32
    ).astype(jnp.bfloat16)
    joined = jnp.concatenate([dense_out, pair_values], axis=1)
    grad_in = lax.dot_general(
        top_cotangent, top_weight, (((1,), (1,)), ((), ())), preferred_element_type=jnp.float32
    )
    top_part = lax.dot_general(
        joined, top_cotangent, (((0,), (0,)), ((), ())), preferred_element_type=jnp.float32
    )
    bias_part = jnp.sum(top_cotangent, axis=0, dtype=jnp.float32)
    pair_grad = grad_in[:, emb_width:]
    mirror = jnp.dot(
        pair_grad, mirrored, precision=highest, preferred_element_type=jnp.float32
    ).reshape(samples, vectors, vectors)
    mirror_high = mirror.astype(jnp.bfloat16)
    mirror_low = (mirror - mirror_high.astype(jnp.float32)).astype(jnp.bfloat16)
    vec_grad = jnp.einsum("bij,bje->bie", mirror_high, stacked, preferred_element_type=jnp.float32)
    vec_grad = vec_grad + jnp.einsum(
        "bij,bje->bie", mirror_low, stacked, preferred_element_type=jnp.float32
    )
    dense_grad = (grad_in[:, :emb_width] + vec_grad[:, 0]).astype(jnp.bfloat16)
    pooled_grad = vec_grad[:, 1:].astype(jnp.bfloat16)
    row_span = R_SHARD // replicas
    blocks = replicas * shards
    per_block = 2 * samples * lookups // blocks
    count_here = samples * lookups
    capacity = blocks * per_block
    by_table = jnp.transpose(indices, (1, 0, 2)).reshape(tables, count_here)
    lookup_rows = jnp.broadcast_to(
        jnp.transpose(pooled_grad, (1, 0, 2))[:, :, None, :], (tables, samples, lookups, emb_width)
    ).reshape(tables, count_here, emb_width)

    def place_table(member):
        table_keys, table_rows = member
        block_row = table_keys // row_span
        later = lax.broadcasted_iota(jnp.int32, (count_here, count_here), 0)
        sooner = lax.broadcasted_iota(jnp.int32, (count_here, count_here), 1)
        earlier = (block_row[None, :] == block_row[:, None]) & (sooner < later)
        slot_row = block_row * per_block + jnp.sum(earlier, axis=1, dtype=jnp.int32)
        levels = lax.broadcasted_iota(jnp.int32, (capacity, count_here), 0)
        placed = levels == slot_row[None, :]
        rows_out = jnp.dot(
            placed.astype(jnp.bfloat16), table_rows, preferred_element_type=jnp.float32
        ).astype(jnp.bfloat16)
        keys_out = (
            jnp.sum(
                jnp.where(placed, (table_keys % R_SHARD + 1)[None, :], 0), axis=1, dtype=jnp.int32
            )
            - 1
        )
        return (rows_out, keys_out)

    send_rows, send_keys = lax.map(place_table, (by_table, lookup_rows))
    top_grad, bias_grad = lax.psum((top_part, bias_part), ("rep", "shard"))
    grouped_rows = send_rows.reshape(tables, shards, replicas * per_block, emb_width)
    grouped_keys = send_keys.reshape(tables, shards, replicas * per_block)
    partial_value = one_hot_sums(
        lax.all_to_all(grouped_rows, "shard", split_axis=1, concat_axis=1, tiled=True),
        lax.all_to_all(grouped_keys, "shard", split_axis=1, concat_axis=1, tiled=True),
        R_SHARD,
    )
    table_grad = lax.psum(partial_value, "rep")
    return (dense_grad, top_grad, bias_grad, table_grad)


def solution(mesh):
    return jax.shard_map(
        on_device,
        mesh=mesh,
        in_specs=(
            P(("rep", "shard"), None),
            P(("rep", "shard"), None, None),
            P(),
            P(("rep", "shard"), None),
            P(("rep", "shard"), None, None),
        ),
        out_specs=(P(("rep", "shard"), None), P(), P(), P(None, "shard", None)),
        check_vma=False,
    )
```

profile of v0, /device:TPU:0, one launch (start us, length us, event | category | flops | bytes accessed | tf_op | source)
XLA Modules:
  0.0 386.4 jit_solution(17738884548787175198)
XLA Ops:
  9.8 2.0 fusion.17
  17.7 2.8 copy.78
  20.6 2.4 copy.77
  24.8 2.9 copy.79
  27.7 2.2 add.78
  34.0 2.4 broadcast_in_dim.67
  36.3 57.8 %while.25 = (s32[]{:T(128)}, bf16[26,512,128]{2,1,0:T(8,128)(2,1)}, s32[26,512]{1,0:T(8,128)S(1)}, s32[26,256]{1,0:T(8,128)S(1)}, bf16[26,256,128]{2,1,0:T(8,128)(2,1)}, /*index=5*/s32[]{:T(128)}, s32[]{:T(128)}) while((s32[]{:T(128)}, bf16[26,512,128]{2,1,0:T(8,128)(2,1)}, s32[26,512]{1,0:T(8,128)S(1)}, s32[26,256]{1,0:T(8,128)S(1)}, ...), condition=%wide.region_6.7_spmd, body=%wide.region_3.6_spmd.sunk | while | flops 34486784 | bytes 224341 | solution.py:100
  95.0 7.3 %all-to-all-start = ((s32[8,1,1664]{2,1,0:T(1,128)}), s32[8,1,1664]{2,1,0:T(1,128)S(1)}, u32[]{:S(2)}, u32[]{:S(2)}) async-start(s32[8,1,1664]{2,1,0:T(1,128)} %reshape.98), calls=%async_computation | async-start | bytes 106496 | tf_op jit(solution)/shard_map/all_to_all | solution.py:106
  102.3 4.8 %copy.87 = bf16[26,8,64,128]{3,2,0,1:T(8,128)(2,1)} copy(bf16[26,8,64,128]{3,2,1,0:T(8,128)(2,1)} %bitcast.71) | data formatting | bytes 6815744 | tf_op jit(solution)/shard_map/reshape | solution.py:102
  107.1 2.0 all-to-all-done
  109.1 4.5 %all-to-all-start.1 = ((bf16[26,8,64,128]{3,2,0,1:T(8,128)(2,1)}), bf16[26,8,64,128]{3,2,0,1:T(8,128)(2,1)}, u32[]{:S(2)}, u32[]{:S(2)}) async-start(bf16[26,8,64,128]{3,2,0,1:T(8,128)(2,1)} %copy.87), calls=%async_computation.1 | async-start | bytes 6815744 | tf_op jit(solution)/shard_map/all_to_all | solution.py:105
  114.5 2.0 fusion.14
  116.5 2.9 reshape.97
  119.4 2.0 convolution_convert_fusion.1
  124.8 73.4 %all-to-all-done.1 = bf16[26,8,64,128]{3,2,0,1:T(8,128)(2,1)} async-done(((bf16[26,8,64,128]{3,2,0,1:T(8,128)(2,1)}), bf16[26,8,64,128]{3,2,0,1:T(8,128)(2,1)}, u32[]{:S(2)}, u32[]{:S(2)}) %all-to-all-start.1) | async-done | bytes 3407904 | tf_op jit(solution)/shard_map/all_to_all | solution.py:105
  198.2 4.8 %copy.88 = bf16[26,8,64,128]{3,2,1,0:T(8,128)(2,1)} copy(bf16[26,8,64,128]{3,2,0,1:T(8,128)(2,1)} %all-to-all-done.1) | data formatting | bytes 6815744 | tf_op jit(solution)/shard_map/all_to_all | solution.py:105
  203.0 47.0 %while.26 = (s32[]{:T(128)}, f32[26,256,128]{2,1,0:T(8,128)}, s32[26,512]{1,0:T(8,128)S(1)}, bf16[26,512,128]{2,1,0:T(8,128)(2,1)}, s32[]{:T(128)}) while((s32[]{:T(128)}, f32[26,256,128]{2,1,0:T(8,128)}, s32[26,512]{1,0:T(8,128)S(1)}, bf16[26,512,128]{2,1,0:T(8,128)(2,1)}, s32[]{:T(128)}) %tuple.72), condition=%wide.region_8.9_spmd, body=%wide.region_7.8_spmd.sunk | while | flops 33685504 | bytes 269377 | solution.py:22
  219.3 1.8 fusion.47
  226.5 1.8 fusion.47
  237.3 1.8 fusion.47
  251.6 38.0 %psum.22 = f32[1024]{0:T(1024)} all-reduce(f32[1024]{0:T(1024)S(1)} %convert_reduce_fusion.1), channel_id=1, replica_groups=mesh['rep'=4,'shard'=8] {'rep','shard'}, use_global_device_ids=true, to_apply=%region_2.3 | all-reduce | flops 1024 | bytes 8192 | tf_op jit(solution)/shard_map/psum | solution.py:101
  289.6 10.4 %all-reduce.3.cloned.1.call-done = f32[479,1024]{1,0:T(8,128)} async-done(((f32[479,1024]{1,0:T(8,128)}), f32[479,1024]{1,0:T(8,128)}) %all-reduce.3.cloned.1.call-update) | async-done | bytes 1962000 | tf_op jit(solution)/shard_map/psum | solution.py:101
  300.1 74.5 %all-reduce.5.cloned.1.call-done = f32[26,256,128]{2,1,0:T(8,128)} async-done(((f32[26,256,128]{2,1,0:T(8,128)}), f32[26,256,128]{2,1,0:T(8,128)}) %all-reduce.5.cloned.1.call-update) | async-done | bytes 3407888 | tf_op jit(solution)/shard_map/psum | solution.py:109
  374.6 3.2 copy.115
  (334 shorter events, 121.2 us)
Async XLA Ops:
  7.2 1.2 copy-start
  7.2 2.6 copy-start.5
  11.8 4.1 %copy-start.7 = (bf16[128,128]{1,0:T(8,128)(2,1)S(1)}, bf16[128,128]{1,0:T(8,128)(2,1)}, u32[]{:S(2)}) copy-start(bf16[128,128]{1,0:T(8,128)(2,1)} %param.11) | copy-start | bytes 98308
  29.9 1.3 copy-start.1
  31.1 2.6 copy-start.8
  95.0 14.1 %all-to-all-start = ((s32[8,1,1664]{2,1,0:T(1,128)}), s32[8,1,1664]{2,1,0:T(1,128)S(1)}, u32[]{:S(2)}, u32[]{:S(2)}) async-start(s32[8,1,1664]{2,1,0:T(1,128)} %reshape.98), calls=%async_computation | async-start | bytes 106496 | tf_op jit(solution)/shard_map/all_to_all | solution.py:106
  109.1 89.1 %all-to-all-start.1 = ((bf16[26,8,64,128]{3,2,0,1:T(8,128)(2,1)}), bf16[26,8,64,128]{3,2,0,1:T(8,128)(2,1)}, u32[]{:S(2)}, u32[]{:S(2)}) async-start(bf16[26,8,64,128]{3,2,0,1:T(8,128)(2,1)} %copy.87), calls=%async_computation.1 | async-start | bytes 6815744 | tf_op jit(solution)/shard_map/all_to_all | solution.py:105
  113.6 186.5 %all-reduce.3.cloned.1.call-start = ((), (), s32[]{:S(2)}) async-start(), calls=%async_computation.2 | async-start | bytes 3932160 | tf_op jit(solution)/shard_map/psum | solution.py:101
  114.5 4.9 %copy-start.4 = (f32[729,351]{1,0:T(8,128)S(1)}, f32[729,351]{1,0:T(8,128)}, u32[]{:S(2)}) copy-start(f32[729,351]{1,0:T(8,128)} %constant.104.clone) | copy-start | bytes 3070552
  116.5 4.9 %copy-start.3 = (bf16[128,1024]{1,0:T(8,128)(2,1)S(1)}, bf16[128,1024]{1,0:T(8,128)(2,1)}, u32[]{:S(2)}) copy-start(bf16[128,1024]{1,0:T(8,128)(2,1)} %param.14) | copy-start | bytes 786436
  116.5 4.9 %copy-start.6 = (bf16[128,128]{0,1:T(8,128)(2,1)S(1)}, bf16[128,128]{0,1:T(8,128)(2,1)}, u32[]{:S(2)}) copy-start(bf16[128,128]{0,1:T(8,128)(2,1)} %copy.81) | copy-start | bytes 98308
  123.2 251.4 %all-reduce.5.cloned.1.call-start = ((), (), s32[]{:S(2)}) async-start(), calls=%async_computation.3 | async-start | bytes 6815744 | tf_op jit(solution)/shard_map/psum | solution.py:109
  374.6 3.2 copy-start.2
Sparse Core Ops, SparseCore 0:
  123.3 176.7 all-reduce.2
  303.0 71.5 all-reduce.4
where the time goes:
time: 389 us; the launch traced here: 386 us
  waiting for transfers between devices  160 us (41%)
  matrix products  105 us (27%)
  local copies, waits for them, and re-layouts  41.3 us (11%)
  blocking collectives  38 us (10%)
  other arithmetic  14.6 us (4%)
  between operations  14.3 us (4%)
  starting transfers between devices  12 us (3%)
    psum x1, waiting for transfers between devices, on_device(): table_grad = lax.psum(partial_value, 'rep')  74.5 us
    all_to_all x1, waiting for transfers between devices, on_device(): lax.all_to_all(grouped_rows, 'shard', split_axis=1, concat_axis=1, tiled=...  73.4 us
    dot_general x26, matrix products, per_table(): return jnp.dot(matches, table_rows, preferred_element_type=jnp.float32)  46.8 us
    dot_general x26, matrix products, place_table(): jnp.dot(placed.astype(jnp.bfloat16), table_rows, preferred_element_type=j...  45.3 us
    psum x1, blocking collectives, on_device(): top_grad, bias_grad = lax.psum((top_part, bias_part), ('rep', 'shard'))  38 us
    unnamed x25, local copies, waits for them, and re-layouts  11.4 us
    psum x1, waiting for transfers between devices, on_device(): top_grad, bias_grad = lax.psum((top_part, bias_part), ('rep', 'shard'))  10.4 us
  transfers between devices with their start and end apart: 4, of which 4 were waited for; matrix products, arithmetic and copies ran while one was open for 18% of the time, Pallas kernels for 0%

commit v1 on v0

--- a/solution.py
+++ b/solution.py
@@ -106,7 +106,12 @@
         lax.all_to_all(grouped_keys, "shard", split_axis=1, concat_axis=1, tiled=True),
         R_SHARD,
     )
-    table_grad = lax.psum(partial_value, "rep")
+    num_devices = lax.axis_size("rep")
+    table_grad = partial_value
+    for h in [
+        [(c, c ^ k) for c in range(num_devices)] for k in (1, 2, 4, 8, 16) if k < num_devices
+    ]:
+        table_grad = table_grad + lax.ppermute(table_grad, axis_name="rep", perm=h)
     return (dense_grad, top_grad, bias_grad, table_grad)
 
 

time: 389 us -> 407 us (1.046)
  blocking collectives: 38 us -> 103 us
  waiting for transfers between devices: 160 us -> 105 us
  other arithmetic: 14.6 us -> 24 us
    psum x1 -> x0, waiting for transfers between devices: 74.5 us -> none  [on_device(): table_grad = lax.psum(partial_value, 'rep')]
    psum x1, blocking collectives: 38 us -> 103 us  [on_device(): top_grad, bias_grad = lax.psum((top_part, bias_part), ('rep', 'shard'))]
    psum x1, waiting for transfers between devices: 10.4 us -> 23.2 us  [on_device(): top_grad, bias_grad = lax.psum((top_part, bias_part), ('rep', 'shard'))]
    add x0 -> x2, other arithmetic: none -> 9.44 us  [on_device(): table_grad = table_grad + lax.ppermute(table_grad, axis_name='rep', perm=h)]
    ppermute x0 -> x2, waiting for transfers between devices: none -> 6.24 us  [on_device(): table_grad = table_grad + lax.ppermute(table_grad, axis_name='rep', perm=h)]
    unnamed x25 -> x20, local copies, waits for them, and re-layouts: 11.4 us -> 8.86 us
  transfers between devices with their start and end apart: 4 -> 5, of which waited for: 4 -> 4; matrix products, arithmetic and copies ran while one was open for 18% -> 5% of each run, Pallas kernels for 0% -> 0%
where the time goes in v1:
time: 407 us; the launch traced here: 404 us
  matrix products  105 us (26%)
  waiting for transfers between devices  105 us (26%)
  blocking collectives  103 us (25%)
  local copies, waits for them, and re-layouts  38.8 us (10%)
  other arithmetic  24 us (6%)
  between operations  14.3 us (4%)
  starting transfers between devices  13.5 us (3%)
    psum x1, blocking collectives, on_device(): top_grad, bias_grad = lax.psum((top_part, bias_part), ('rep', 'shard'))  103 us
    all_to_all x1, waiting for transfers between devices, on_device(): lax.all_to_all(grouped_rows, 'shard', split_axis=1, concat_axis=1, tiled=...  73.6 us
    dot_general x26, matrix products, per_table(): return jnp.dot(matches, table_rows, preferred_element_type=jnp.float32)  46.8 us
    dot_general x26, matrix products, place_table(): jnp.dot(placed.astype(jnp.bfloat16), table_rows, preferred_element_type=j...  45.3 us
    psum x1, waiting for transfers between devices, on_device(): top_grad, bias_grad = lax.psum((top_part, bias_part), ('rep', 'shard'))  23.2 us
    add x2, other arithmetic, on_device(): table_grad = table_grad + lax.ppermute(table_grad, axis_name='rep', perm=h)  9.44 us
    unnamed x20, local copies, waits for them, and re-layouts  8.86 us
  transfers between devices with their start and end apart: 5, of which 4 were waited for; matrix products, arithmetic and copies ran while one was open for 5% of the time, Pallas kernels for 0%

profile of v1, /device:TPU:0, one launch (start us, length us, event | category | flops | bytes accessed | tf_op | source)
XLA Modules:
  0.0 404.2 jit_solution(3883946638529452408)
XLA Ops:
  9.8 2.0 fusion.17
  17.7 2.8 copy.78
  20.6 2.4 copy.77
  24.8 2.9 copy.79
  27.7 2.2 add.82
  33.9 2.4 broadcast_in_dim.67
  36.3 57.8 %while.25 = (s32[]{:T(128)}, bf16[26,512,128]{2,1,0:T(8,128)(2,1)}, s32[26,512]{1,0:T(8,128)S(1)}, s32[26,256]{1,0:T(8,128)S(1)}, bf16[26,256,128]{2,1,0:T(8,128)(2,1)}, /*index=5*/s32[]{:T(128)}, s32[]{:T(128)}) while((s32[]{:T(128)}, bf16[26,512,128]{2,1,0:T(8,128)(2,1)}, s32[26,512]{1,0:T(8,128)S(1)}, s32[26,256]{1,0:T(8,128)S(1)}, ...), condition=%wide.region_6.7_spmd, body=%wide.region_3.6_spmd.sunk | while | flops 34486784 | bytes 224341 | solution.py:100
  95.0 7.3 %all-to-all-start = ((s32[8,1,1664]{2,1,0:T(1,128)}), s32[8,1,1664]{2,1,0:T(1,128)S(1)}, u32[]{:S(2)}, u32[]{:S(2)}) async-start(s32[8,1,1664]{2,1,0:T(1,128)} %reshape.98), calls=%async_computation | async-start | bytes 106496 | tf_op jit(solution)/shard_map/all_to_all | solution.py:106
  102.3 4.8 %copy.87 = bf16[26,8,64,128]{3,2,0,1:T(8,128)(2,1)} copy(bf16[26,8,64,128]{3,2,1,0:T(8,128)(2,1)} %bitcast.71) | data formatting | bytes 6815744 | tf_op jit(solution)/shard_map/reshape | solution.py:102
  107.1 2.0 all-to-all-done
  109.1 4.5 %all-to-all-start.1 = ((bf16[26,8,64,128]{3,2,0,1:T(8,128)(2,1)}), bf16[26,8,64,128]{3,2,0,1:T(8,128)(2,1)}, u32[]{:S(2)}, u32[]{:S(2)}) async-start(bf16[26,8,64,128]{3,2,0,1:T(8,128)(2,1)} %copy.87), calls=%async_computation.1 | async-start | bytes 6815744 | tf_op jit(solution)/shard_map/all_to_all | solution.py:105
  115.3 73.6 %all-to-all-done.1 = bf16[26,8,64,128]{3,2,0,1:T(8,128)(2,1)} async-done(((bf16[26,8,64,128]{3,2,0,1:T(8,128)(2,1)}), bf16[26,8,64,128]{3,2,0,1:T(8,128)(2,1)}, u32[]{:S(2)}, u32[]{:S(2)}) %all-to-all-start.1) | async-done | bytes 3407904 | tf_op jit(solution)/shard_map/all_to_all | solution.py:105
  188.9 4.8 %copy.88 = bf16[26,8,64,128]{3,2,1,0:T(8,128)(2,1)} copy(bf16[26,8,64,128]{3,2,0,1:T(8,128)(2,1)} %all-to-all-done.1) | data formatting | bytes 6815744 | tf_op jit(solution)/shard_map/all_to_all | solution.py:105
  193.7 47.0 %while.26 = (s32[]{:T(128)}, f32[26,256,128]{2,1,0:T(8,128)}, s32[26,512]{1,0:T(8,128)S(1)}, bf16[26,512,128]{2,1,0:T(8,128)(2,1)}, s32[]{:T(128)}) while((s32[]{:T(128)}, f32[26,256,128]{2,1,0:T(8,128)}, s32[26,512]{1,0:T(8,128)S(1)}, bf16[26,512,128]{2,1,0:T(8,128)(2,1)}, s32[]{:T(128)}) %tuple.70), condition=%wide.region_8.9_spmd, body=%wide.region_7.8_spmd.sunk | while | flops 33685504 | bytes 269377 | solution.py:22
  195.6 1.8 fusion.47
  240.7 6.2 %collective-permute-done = f32[26,256,128]{2,1,0:T(8,128)S(1)} collective-permute-done((f32[26,256,128]{2,1,0:T(8,128)}, f32[26,256,128]{2,1,0:T(8,128)S(1)}, u32[]{:S(2)}, u32[]{:S(2)}) %collective-permute-start) | collective-permute-done | bytes 3407904 | tf_op jit(solution)/shard_map/ppermute | solution.py:114
  247.0 4.2 %add.84 = f32[26,256,128]{2,1,0:T(8,128)} add(f32[26,256,128]{2,1,0:T(8,128)} %get-tuple-element.119, f32[26,256,128]{2,1,0:T(8,128)S(1)} %collective-permute-done) | non-fusion elementwise | flops 851968 | bytes 10223616 | tf_op jit(solution)/shard_map/add | solution.py:114
  252.7 2.0 fusion.14
  254.8 2.9 reshape.97
  257.7 2.0 convolution_convert_fusion.1
  263.0 102.8 %psum.15 = f32[1024]{0:T(1024)} all-reduce(f32[1024]{0:T(1024)S(1)} %convert_reduce_fusion.1), channel_id=1, replica_groups=mesh['rep'=4,'shard'=8] {'rep','shard'}, use_global_device_ids=true, to_apply=%region_2.3 | all-reduce | flops 1024 | bytes 8192 | tf_op jit(solution)/shard_map/psum | solution.py:101
  365.8 5.3 %add.85 = f32[26,256,128]{2,1,0:T(8,128)} add(f32[26,256,128]{2,1,0:T(8,128)} %add.84, f32[26,256,128]{2,1,0:T(8,128)} %collective-permute-done.1) | non-fusion elementwise | flops 851968 | bytes 10223616 | tf_op jit(solution)/shard_map/add | solution.py:114
  371.1 23.2 %all-reduce.2.cloned.1.call-done = f32[479,1024]{1,0:T(8,128)} async-done(((f32[479,1024]{1,0:T(8,128)}), f32[479,1024]{1,0:T(8,128)}) %all-reduce.2.cloned.1.call-update) | async-done | bytes 1962000 | tf_op jit(solution)/shard_map/psum | solution.py:101
  394.3 3.0 copy.114
  (332 shorter events, 123.8 us)
Async XLA Ops:
  7.2 1.2 copy-start
  7.2 2.6 copy-start.4
  11.8 4.1 %copy-start.5 = (bf16[128,128]{1,0:T(8,128)(2,1)S(1)}, bf16[128,128]{1,0:T(8,128)(2,1)}, u32[]{:S(2)}) copy-start(bf16[128,128]{1,0:T(8,128)(2,1)} %param.11) | copy-start | bytes 98308
  29.9 1.2 copy-start.1
  31.1 2.6 copy-start.6
  95.0 14.1 %all-to-all-start = ((s32[8,1,1664]{2,1,0:T(1,128)}), s32[8,1,1664]{2,1,0:T(1,128)S(1)}, u32[]{:S(2)}, u32[]{:S(2)}) async-start(s32[8,1,1664]{2,1,0:T(1,128)} %reshape.98), calls=%async_computation | async-start | bytes 106496 | tf_op jit(solution)/shard_map/all_to_all | solution.py:106
  109.1 79.8 %all-to-all-start.1 = ((bf16[26,8,64,128]{3,2,0,1:T(8,128)(2,1)}), bf16[26,8,64,128]{3,2,0,1:T(8,128)(2,1)}, u32[]{:S(2)}, u32[]{:S(2)}) async-start(bf16[26,8,64,128]{3,2,0,1:T(8,128)(2,1)} %copy.87), calls=%async_computation.1 | async-start | bytes 6815744 | tf_op jit(solution)/shard_map/all_to_all | solution.py:105
  113.6 280.7 %all-reduce.2.cloned.1.call-start = ((), (), s32[]{:S(2)}) async-start(), calls=%async_computation.2 | async-start | bytes 3932160 | tf_op jit(solution)/shard_map/psum | solution.py:101
  240.7 6.2 %collective-permute-start = (f32[26,256,128]{2,1,0:T(8,128)}, f32[26,256,128]{2,1,0:T(8,128)S(1)}, u32[]{:S(2)}, u32[]{:S(2)}) collective-permute-start(f32[26,256,128]{2,1,0:T(8,128)} %get-tuple-element.119), channel_id=1, source_target_pairs={{0,8},{8,0},{16,24},{24,16},{1,9},{9,1},{17,25},{25,17},{2,10},{10... | collective-permute-start | bytes 10223624 | tf_op jit(solution)/shard_map/ppermute | solution.py:114
  251.1 114.7 %collective-permute-start.1 = (f32[26,256,128]{2,1,0:T(8,128)}, f32[26,256,128]{2,1,0:T(8,128)}, u32[]{:S(2)}, u32[]{:S(2)}) collective-permute-start(f32[26,256,128]{2,1,0:T(8,128)} %add.84), channel_id=1, source_target_pairs={{0,16},{8,24},{16,0},{24,8},{1,17},{9,25},{17,1},{25,9},{2,18},{10... | collective-permute-start | bytes 10223624 | tf_op jit(solution)/shard_map/ppermute | solution.py:114
  252.7 4.9 %copy-start.3 = (f32[729,351]{1,0:T(8,128)S(1)}, f32[729,351]{1,0:T(8,128)}, u32[]{:S(2)}) copy-start(f32[729,351]{1,0:T(8,128)} %constant.104.clone) | copy-start | bytes 3070552
  254.8 4.9 %copy-start.2 = (bf16[128,1024]{1,0:T(8,128)(2,1)S(1)}, bf16[128,1024]{1,0:T(8,128)(2,1)}, u32[]{:S(2)}) copy-start(bf16[128,1024]{1,0:T(8,128)(2,1)} %param.14) | copy-start | bytes 786436
Sparse Core Ops, SparseCore 0:
  261.5 132.7 all-reduce.1
